TPU v7x, 32 devices: a whole 2x2x4 slice. The times are simulated.
32 devices in a mesh: dp: 2 (over core), vocab: 16 (over z, y, x).
Axes of the slice: x: 2, y: 2, z: 4, core: 2. Of those that a mesh axis runs over, the one named last changes fastest.
Arguments:
- table: bfloat16 [16384, 4096], P('vocab'), may hold values from -0.75 to 0.75
- hidden: bfloat16 [512, 4096], P(('dp', 'vocab')), may hold values from -9 to 9
- cotangent: bfloat16 [512, 4096], P(('dp', 'vocab')), may hold values from -0.75 to 0.75
- input_ids: int32 [512], P('dp'), may hold values from 0 to 16383, as said below
- target_ids: int32 [512], P('dp'), may hold values from 0 to 16383
Outputs:
- table_grad: float32 [16384, 4096], P(('vocab', 'dp'))
- hidden_grad: bfloat16 [512, 4096], P(('dp', 'vocab'))
- token_loss: float32 [512], P('dp')
Inputs may be any that keep to these rules, and one draw needn't show every extreme that they name: `input_ids`: the ids of one replica group may all lie in the 1024 rows of one index of vocab; in every draw some group's ids do.
All inputs are finite; a program needn't handle non-finite values.
Results may differ from a plain program's by a relative error of at most 0.0034.
Values may be sent and summed in bfloat16 or wider, within the bound.
A program may use at most 128 MiB of HBM per device.

v0:
```python
import functools

import jax
import jax.numpy as jnp
from jax import lax
from jax.experimental import pallas as pl
from jax.experimental.pallas import tpu as pltpu
from jax.sharding import PartitionSpec as P

MESH = pl.DeviceIdType.MESH
BF16 = jnp.bfloat16
F32 = jnp.float32
WIRE1 = BF16
WIRE2 = BF16
WIREZ = BF16
CHUNKS = 2


def kernel(groups, n, table_hbm, hidden_ref, cot_ref, in_ids_ref, tgt_ids_ref,
           x_all, e_all, hg_ref, loss_ref,
           table, x_own, logits, st, own_e, part, s1, r1, s2, r2, s3, r3,
           load_sem, local_sem, send, recv):
    nz = n // 4
    rows, width = hidden_ref.shape
    shard = table.shape[0]
    tokens = n * rows
    piece = shard // groups
    half = width // 2
    me = lax.axis_index("vocab")
    g = lax.axis_index("dp")
    z = me // 4
    y = (me % 4) // 2
    x = me % 2
    slots = iter(range(send.shape[0]))

    def at(zz, yy, xx):
        return zz * 4 + yy * 2 + xx

    x_peer = at(z, y, 1 - x)
    y_peer = at(z, 1 - y, x)

    load = pltpu.make_async_copy(table_hbm, table, load_sem)
    load.start()

    barrier = pltpu.get_barrier_semaphore()
    for d in range(1, n):
        pl.semaphore_signal(barrier, inc=1, device_id=(g, (me + d) % n), device_id_type=MESH)
    for d in range(1, groups):
        pl.semaphore_signal(barrier, inc=1, device_id=((g + d) % groups, me), device_id_type=MESH)
    pl.semaphore_wait(barrier, n - 1 + groups - 1)

    started = []

    def when(cond, act):
        if cond is None:
            act()
        else:
            pl.when(cond)(act)

    def both(a, b):
        return b if a is None else jnp.logical_and(a, b)

    def push(src, dst, v, gg=None, cond=None):
        k = next(slots)
        c = pltpu.make_async_remote_copy(
            src_ref=src, dst_ref=dst, send_sem=send.at[k], recv_sem=recv.at[k],
            device_id=(g if gg is None else gg, v), device_id_type=MESH)
        when(cond, c.start)
        started.append((cond, c))
        return c

    above, below = z + 1 < nz, z > 0
    up, down = at(jnp.minimum(z + 1, nz - 1), y, x), at(jnp.maximum(z - 1, 0), y, x)

    def gather_first(kind, own, base, span):
        own = own.at[:, pl.ds(base, span)]
        dst = x_own.at[kind, me, :, pl.ds(base, span)]
        ups = push(own, dst, up, cond=above)
        downs = push(own, dst, down, cond=below)
        return [(None, z, push(own, dst, x_peer), push(own, dst, y_peer))], ups, downs, kind, base, span

    def gather_second(state):
        seen, ups, downs, kind, base, span = state
        for s in range(nz - 1):
            for inward, cond, zz, go, nxt in ((ups, z - 1 - s >= 0, jnp.maximum(z - 1 - s, 0), above, up),
                                              (downs, z + 1 + s < nz, jnp.minimum(z + 1 + s, nz - 1), below, down)):
                when(cond, inward.wait_recv)
                blk = x_own.at[kind, at(zz, y, x), :, pl.ds(base, span)]
                if s < nz - 2:
                    c = push(blk, blk, nxt, cond=both(cond, go))
                    if nxt is up:
                        ups = c
                    else:
                        downs = c
                seen.append((cond, zz, push(blk, blk, x_peer, cond=cond), push(blk, blk, y_peer, cond=cond)))

    def gather_third(state):
        seen, _, _, kind, base, span = state
        left = pl.ds(base, span // 2)
        right = pl.ds(base + span // 2, span // 2)
        out = []
        for cond, zz, fx, fy in seen:
            when(cond, fx.wait_recv)
            blk = x_own.at[kind, at(zz, y, 1 - x), :, left]
            out.append((cond, push(blk, blk, y_peer, cond=cond)))
            when(cond, fy.wait_recv)
            blk = x_own.at[kind, at(zz, 1 - y, x), :, right]
            out.append((cond, push(blk, blk, x_peer, cond=cond)))
        return out

    local = []

    def spread(kind):
        c = pltpu.make_async_copy(x_own.at[kind], x_all.at[g, kind], local_sem.at[kind])
        c.start()
        local.append(c)
        return [push(x_own.at[kind], x_all.at[g, kind], me, (g + d) % groups) for d in range(1, groups)]

    states = [gather_first(0, hidden_ref, i * half, half) for i in range(2)]
    x_own[0, pl.ds(me, 1)] = hidden_ref[...][None]
    x_own[1, pl.ds(me, 1)] = cot_ref[...][None]
    tails = []
    for state in states:
        gather_second(state)
        tails.append(gather_third(state))
    cot_state = gather_first(1, cot_ref, 0, width)
    offset = me * shard
    step = 256
    for i in range(0, shard, step):
        vocab_row = offset + i + lax.broadcasted_iota(jnp.int32, (step, tokens), 0)
        own_e[1, i:i + step] = (vocab_row == in_ids_ref[...]).astype(F32).astype(BF16)
    load.wait()
    top = jnp.full((1, tokens), -jnp.inf, F32)
    for k in range(2):
        for cond, c in tails[k]:
            when(cond, c.wait_recv)
        h = x_own[0, :, :, k * half:(k + 1) * half].reshape(tokens, half)
        for i in range(0, shard, step):
            lg = lax.dot_general(table[i:i + step, k * half:(k + 1) * half], h, (((1,), (1,)), ((), ())),
                                 preferred_element_type=F32)
            if k == 1:
                lg = lg + logits[i:i + step]
                top = jnp.maximum(top, jnp.max(lg, axis=0, keepdims=True))
            logits[i:i + step] = lg
    late = spread(0)
    total = jnp.zeros((1, tokens), F32)
    pick = jnp.zeros((1, tokens), F32)
    tgt = tgt_ids_ref[...]
    for i in range(0, shard, step):
        lg = logits[i:i + step]
        vocab_row = offset + i + lax.broadcasted_iota(jnp.int32, (step, tokens), 0)
        total = total + jnp.sum(jnp.exp(lg - top), axis=0, keepdims=True)
        pick = pick + jnp.sum(jnp.where(vocab_row == tgt, lg, 0.0), axis=0, keepdims=True)
    line = lax.broadcasted_iota(jnp.int32, (8, tokens), 0)
    mine = jnp.where(line == 0, top, jnp.where(line == 1, total, pick))
    st[pl.ds(me, 1)] = mine[None]
    stats = [push(st.at[me], st.at[me], (me + d) % n) for d in range(1, n)]
    gather_second(cot_state)
    for c in stats:
        c.wait_recv()
    top = st[0, 0:1]
    for j in range(1, n):
        top = jnp.maximum(top, st[j, 0:1])
    total = jnp.zeros((1, tokens), F32)
    pick = jnp.zeros((1, tokens), F32)
    for j in range(n):
        total = total + st[j, 1:2] * jnp.exp(st[j, 0:1] - top)
        pick = pick + st[j, 2:3]
    lse = top + jnp.log(total)
    loss_ref[...] = lse - pick
    for i in range(0, shard, step):
        vocab_row = offset + i + lax.broadcasted_iota(jnp.int32, (step, tokens), 0)
        hit = (vocab_row == tgt).astype(F32)
        own_e[0, i:i + step] = (jnp.exp(logits[i:i + step] - lse) - hit).astype(BF16)

    dl = own_e[0]
    cols = 512

    def product(i):
        p = lax.dot_general(dl, table[:, i:i + cols], (((0,), (0,)), ((), ())), preferred_element_type=F32)
        part[:, :, :, :, i:i + cols] = p.reshape(nz, 2, 2, rows, cols)

    wide = half // CHUNKS
    firsts = [[], []]
    for c in range(CHUNKS):
        for side in range(2):
            lo = side * half + c * wide
            for i in range(lo, lo + wide, cols):
                product(i)
            if side == 0:
                p = part[:, pl.ds(1 - y, 1), :, :, lo:lo + wide]
            else:
                p = part[:, :, pl.ds(1 - x, 1), :, lo:lo + wide]
            s1[side, c] = p.reshape(nz, 2, rows, wide).astype(WIRE1)
            firsts[side].append(push(s1.at[side, c], r1.at[side, c], y_peer if side == 0 else x_peer))

    for kind in range(2):
        dst = e_all.at[:, pl.ds(pl.multiple_of((g * 2 + kind) * tokens, tokens), tokens)]
        c = pltpu.make_async_copy(
            own_e.at[kind, pl.ds(pl.multiple_of(g * piece, piece), piece)], dst, local_sem.at[2 + kind])
        c.start()
        local.append(c)
        for d in range(1, groups):
            peer = (g + d) % groups
            late.append(push(own_e.at[kind, pl.ds(pl.multiple_of(peer * piece, piece), piece)], dst, me, peer))

    def merged_first(side, c, zz, yy, xx, count):
        lo = side * half + c * wide
        a = part[pl.ds(zz, count), pl.ds(yy, 1), pl.ds(xx, 1), :, lo:lo + wide].reshape(count, rows, wide)
        b = r1[side, c, pl.ds(zz, count), pl.ds(xx if side == 0 else yy, 1)].reshape(count, rows, wide)
        return a + b.astype(F32)

    seconds = [[], []]
    for c in range(CHUNKS):
        for side in range(2):
            firsts[side][c].wait_recv()
            yy, xx, peer = (y, 1 - x, x_peer) if side == 0 else (1 - y, x, y_peer)
            s2[side, c] = merged_first(side, c, 0, yy, xx, nz).astype(WIRE2)
            seconds[side].append(push(s2.at[side, c], r2.at[side, c], peer))

    cot_tail = gather_third(cot_state)

    def merged(side, c, zz):
        return (merged_first(side, c, zz, y, x, 1)
                + r2[side, c, pl.ds(zz, 1)].astype(F32)).reshape(rows, wide)

    last = []
    for c in range(CHUNKS):
        for side in range(2):
            seconds[side][c].wait_recv()
            for d in range(1, nz):
                zz = (z + d) % nz
                s3[side, c, d - 1] = merged(side, c, zz).astype(WIREZ)
                last.append(push(s3.at[side, c, d - 1], r3.at[side, c, d - 1], at(zz, y, x)))
    for cond, c in cot_tail:
        when(cond, c.wait_recv)
    late += spread(1)
    for c in last:
        c.wait_recv()
    for c in range(CHUNKS):
        for side in range(2):
            acc = merged(side, c, z)
            for d in range(1, nz):
                acc = acc + r3[side, c, d - 1].astype(F32)
            lo = side * half + c * wide
            hg_ref[:, lo:lo + wide] = acc.astype(BF16)
    for c in late:
        c.wait_recv()
    for c in local:
        c.wait()
    for cond, c in started:
        when(cond, c.wait_send)


def weight_kernel(e_ref, x_ref, out_ref):
    out_ref[...] = jnp.dot(e_ref[...], x_ref[...], preferred_element_type=F32)


def weight_grad(e, x):
    tile = 512
    return pl.pallas_call(
        weight_kernel,
        grid=(x.shape[1] // tile,),
        out_shape=jax.ShapeDtypeStruct((e.shape[0], x.shape[1]), F32),
        in_specs=[
            pl.BlockSpec(e.shape, lambda i: (0, 0)),
            pl.BlockSpec((x.shape[0], tile), lambda i: (0, i)),
        ],
        out_specs=pl.BlockSpec((e.shape[0], tile), lambda i: (0, i)),
        compiler_params=pltpu.CompilerParams(vmem_limit_bytes=60 * 2**20),
    )(e, x)


def solution(mesh):
    groups, n = mesh.shape["dp"], mesh.shape["vocab"]

    def body(table, hidden, cotangent, input_ids, target_ids):
        rows, width = hidden.shape
        shard = table.shape[0]
        nz = n // 4
        tokens = n * rows
        half = width // 2
        piece = shard // groups
        copies = 3 * (4 + 2 * (nz - 2) + 8 * (nz - 1) + 2) + 2 * (groups - 1) + (n - 1) + 2 * (groups - 1) + CHUNKS * (4 + 2 * (nz - 1))
        wide = half // CHUNKS
        vmem = pl.BlockSpec(memory_space=pltpu.VMEM)
        anys = pl.BlockSpec(memory_space=pl.ANY)
        x_all, e_all, hg, loss = pl.pallas_call(
            functools.partial(kernel, groups, n),
            out_shape=(
                jax.ShapeDtypeStruct((groups, 2, n, rows, width), BF16),
                jax.ShapeDtypeStruct((piece, groups * 2 * tokens), BF16),
                jax.ShapeDtypeStruct((rows, width), BF16),
                jax.ShapeDtypeStruct((1, tokens), F32),
            ),
            in_specs=[anys, vmem, vmem, vmem, vmem],
            out_specs=(anys, anys, vmem, vmem),
            scratch_shapes=[
                pltpu.VMEM((shard, width), BF16),
                pltpu.VMEM((2, n, rows, width), BF16),
                pltpu.VMEM((shard, tokens), F32),
                pltpu.VMEM((n, 8, tokens), F32),
                pltpu.VMEM((2, shard, tokens), BF16),
                pltpu.VMEM((nz, 2, 2, rows, width), F32),
                pltpu.VMEM((2, CHUNKS, nz, 2, rows, wide), WIRE1),
                pltpu.VMEM((2, CHUNKS, nz, 2, rows, wide), WIRE1),
                pltpu.VMEM((2, CHUNKS, nz, rows, wide), WIRE2),
                pltpu.VMEM((2, CHUNKS, nz, rows, wide), WIRE2),
                pltpu.VMEM((2, CHUNKS, nz - 1, rows, wide), WIREZ),
                pltpu.VMEM((2, CHUNKS, nz - 1, rows, wide), WIREZ),
                pltpu.SemaphoreType.DMA,
                pltpu.SemaphoreType.DMA((4,)),
                pltpu.SemaphoreType.DMA((copies,)),
                pltpu.SemaphoreType.DMA((copies,)),
            ],
            compiler_params=pltpu.CompilerParams(
                collective_id=0, has_side_effects=True, vmem_limit_bytes=56 * 2**20),
        )(table, hidden, cotangent, input_ids.reshape(1, tokens), target_ids.reshape(1, tokens))
        table_grad = weight_grad(e_all, x_all.reshape(groups * 2 * tokens, width))
        return table_grad, hg, loss.reshape(tokens)

    return jax.shard_map(
        body,
        mesh=mesh,
        in_specs=(
            P("vocab", None),
            P(("dp", "vocab"), None),
            P(("dp", "vocab"), None),
            P("dp"),
            P("dp"),
        ),
        out_specs=(P(("vocab", "dp"), None), P(("dp", "vocab"), None), P("dp")),
        check_vma=False,
    )
```

profile of v0, /device:TPU:0, one launch (start us, length us, event | category | flops | bytes accessed | tf_op | source)
XLA Modules:
  0.0 85.4 jit_solution(11034349734399259251)
XLA Ops:
  0.6 72.4 %shard_map.76 = (bf16[2,2,16,16,4096]{4,3,2,1,0:T(8,128)(2,1)}, bf16[512,1024]{1,0:T(8,128)(2,1)}, bf16[16,4096]{1,0:T(8,128)(2,1)}, f32[1,256]{1,0:T(1,128)}) custom-call(bf16[1024,4096]{1,0:T(8,128)(2,1)} %table_hbm.1, bf16[16,4096]{1,0:T(8,128)(2,1)} %hidden_ref.1, bf16[16,4096]{1,0:T(8,128)(2,1)} %cot_ref.1, s32[1,256]{1,0:T(1,128)} %bitcast.5, ...), custom_call_target="tpu_custom_call" | custom-call | tf_op jit(solution)/shard_map/pallas_call | solution.py:288
  73.0 0.0 copy-start
  73.0 0.0 copy-start.1
  73.0 11.2 %shard_map.77 = f32[512,4096]{1,0:T(8,128)} custom-call(bf16[512,1024]{1,0:T(8,128)(2,1)} %get-tuple-element.7.e_ref, bf16[1024,4096]{1,0:T(8,128)(2,1)} %bitcast.4), custom_call_target="tpu_custom_call" | custom-call | tf_op jit(solution)/shard_map/pallas_call | solution.py:261
  84.2 0.0 copy-done
  84.2 0.7 copy.10
  84.9 0.0 copy-done.1
  84.9 0.6 copy.11
Async XLA Ops:
  73.0 11.2 %copy-start = (bf16[16,4096]{1,0:T(8,128)(2,1)S(1)}, bf16[16,4096]{1,0:T(8,128)(2,1)}, u32[]{:S(2)}) copy-start(bf16[16,4096]{1,0:T(8,128)(2,1)} %get-tuple-element.15) | copy-start | bytes 393220
  73.0 11.8 %copy-start.1 = (f32[1,256]{1,0:T(1,128)S(1)}, f32[1,256]{1,0:T(1,128)}, u32[]{:S(2)}) copy-start(f32[1,256]{1,0:T(1,128)} %get-tuple-element.10) | copy-start | bytes 3076
where the time goes:
time: 85.8 us; the launch traced here: 85.4 us
  Pallas kernels  83.6 us (97%)
  local copies, waits for them, and re-layouts  1.23 us (1%)
    pallas_call x1, Pallas kernels, body(): pl.pallas_call(functools.partial(kernel, groups, n), out_shape=(jax.Shape...  72.4 us
    pallas_call x1, Pallas kernels, weight_grad(): pl.pallas_call(weight_kernel, grid=(x.shape[1] // tile,), out_shape=jax.S...  11.2 us

commit v1 on v0

v1 whole, which is shorter than its diff:
```python
import functools
import math

import jax
import jax.numpy as jnp
from jax import lax
from jax.experimental import pallas as pl
from jax.experimental.pallas import tpu as pltpu
from jax.sharding import PartitionSpec as P

MESH = pl.DeviceIdType.MESH
BF16 = jnp.bfloat16
F32 = jnp.float32
TILE = 512


def chunk_list(half):
    w = half // 4
    return [(i * w, w) for i in range(4)]


def count_copies(groups, n, chunks):
    nz = n // 4
    column = 3 + 2 * (nz - 1) + 2 * (nz - 2)
    first = 4 + 4 * (nz - 1) + 2 * (nz - 2)
    gather = 2 + first + 2 + 4 * (nz - 1) + 4 * column
    return 2 * gather + (n - 1) + 4 * (groups - 1) + chunks * (4 + 2 * (nz - 1))


def kernel(groups, n, table_hbm, hidden_hbm, cot_hbm, in_ids_hbm, tgt_hbm,
           tg_ref, hg_ref, loss_ref,
           table, x_all, logits, st, dl_ref, dlt_ref, e_in, hot, ids, tgt_ref,
           part, s1, r1, s2, r2, s3, r3, load_sem, send, recv):
    nz = n // 4
    rows, width = hg_ref.shape
    shard = table.shape[0]
    tokens = n * rows
    piece = shard // groups
    half = width // 2
    me = lax.axis_index("vocab")
    g = lax.axis_index("dp")
    z = me // 4
    y = (me % 4) // 2
    x = me % 2
    slots = iter(range(send.shape[0]))

    def at(zz, yy, xx):
        return zz * 4 + yy * 2 + xx

    x_peer = at(z, y, 1 - x)
    y_peer = at(z, 1 - y, x)
    above, below = z + 1 < nz, z > 0
    up, down = at(jnp.minimum(z + 1, nz - 1), y, x), at(jnp.maximum(z - 1, 0), y, x)

    def when(cond, act):
        if cond is None:
            act()
        else:
            pl.when(cond)(act)

    barrier = pltpu.get_barrier_semaphore()

    def greet(v, gg=None):
        pl.semaphore_signal(barrier, inc=1, device_id=(g if gg is None else gg, v), device_id_type=MESH)

    greet(x_peer)
    greet(y_peer)
    when(above, lambda: greet(up))
    when(below, lambda: greet(down))
    for d in range(1, groups):
        greet(me, (g + d) % groups)

    loads = [
        pltpu.make_async_copy(hidden_hbm, x_all.at[g, 0, me], load_sem.at[0]),
        pltpu.make_async_copy(cot_hbm, x_all.at[g, 1, me], load_sem.at[1]),
        pltpu.make_async_copy(in_ids_hbm, ids.at[0], load_sem.at[2]),
        pltpu.make_async_copy(tgt_hbm, tgt_ref, load_sem.at[3]),
        pltpu.make_async_copy(table_hbm, table, load_sem.at[4]),
    ]
    for c in loads:
        c.start()
    loads[0].wait()
    pl.semaphore_wait(barrier, 2 + above.astype(jnp.int32) + below.astype(jnp.int32) + groups - 1)

    started = []

    def both(a, b):
        return b if a is None else jnp.logical_and(a, b)

    def push(src, dst, v, gg=None, cond=None):
        k = next(slots)
        c = pltpu.make_async_remote_copy(
            src_ref=src, dst_ref=dst, send_sem=send.at[k], recv_sem=recv.at[k],
            device_id=(g if gg is None else gg, v), device_id_type=MESH)
        when(cond, c.start)
        started.append((cond, c))
        return c

    wa = width * 3 // 8
    wb = width * 5 // 16
    sets = [(0, wa), (wa, wb), (wa + wb, width - wa - wb)]

    class Column:
        def __init__(self, kind, k, yy, xx, fan):
            self.kind, self.cols, self.yy, self.xx, self.fan = kind, pl.ds(*sets[k]), yy, xx, fan
            mine = self.blk(z)
            self.ups = push(mine, mine, up, cond=above)
            self.downs = push(mine, mine, down, cond=below)
            self.seen = [(None, z, [push(mine, mine, p) for p in fan])]

        def blk(self, zz):
            return x_all.at[g, self.kind, at(zz, self.yy, self.xx), :, self.cols]

        def step(self, s):
            ups, downs = self.ups, self.downs
            for inward, cond, zz, go, nxt in ((ups, z - 1 - s >= 0, jnp.maximum(z - 1 - s, 0), above, up),
                                              (downs, z + 1 + s < nz, jnp.minimum(z + 1 + s, nz - 1), below, down)):
                when(cond, inward.wait_recv)
                b = self.blk(zz)
                if s < nz - 2:
                    c = push(b, b, nxt, cond=both(cond, go))
                    if nxt is up:
                        self.ups = c
                    else:
                        self.downs = c
                self.seen.append((cond, zz, [push(b, b, p, cond=cond) for p in self.fan]))

    finals = [[None] * 3, [None] * 3]

    def gather(kind):
        def own(k):
            return x_all.at[g, kind, me, :, pl.ds(*sets[k])]

        fb = push(own(1), own(1), x_peer)
        fc = push(own(2), own(2), y_peer)
        a = Column(kind, 0, y, x, [x_peer, y_peer])
        b1 = Column(kind, 1, y, x, [y_peer])
        c1 = Column(kind, 2, y, x, [x_peer])
        thirds = []

        def third(items):
            lo, span = sets[0]
            for cond, zz, (fx, fy) in items:
                when(cond, fx.wait_recv)
                b = x_all.at[g, kind, at(zz, y, 1 - x), :, pl.ds(lo, span // 2)]
                thirds.append((cond, push(b, b, y_peer, cond=cond)))
                when(cond, fy.wait_recv)
                b = x_all.at[g, kind, at(zz, 1 - y, x), :, pl.ds(lo + span // 2, span // 2)]
                thirds.append((cond, push(b, b, x_peer, cond=cond)))

        yield
        fb.wait_recv()
        b2 = Column(kind, 1, y, 1 - x, [y_peer])
        fc.wait_recv()
        c2 = Column(kind, 2, 1 - y, x, [x_peer])
        yield
        done = 0
        for s in range(nz - 1):
            new = len(a.seen)
            for col in (a, b1, c1, b2, c2):
                col.step(s)
            third(a.seen[done:new])
            done = new
            yield
        third(a.seen[done:])
        finals[kind] = [
            thirds,
            [(cond, c) for col in (b1, b2) for cond, _, cs in col.seen for c in cs],
            [(cond, c) for col in (c1, c2) for cond, _, cs in col.seen for c in cs],
        ]
        yield

    def land(kind, k):
        for cond, c in finals[kind][k]:
            when(cond, c.wait_recv)

    late = []

    def spread(kind):
        for d in range(1, groups):
            late.append(push(x_all.at[g, kind], x_all.at[g, kind], me, (g + d) % groups))

    g0 = gather(0)
    for _ in g0:
        pass
    loads[1].wait()
    g1 = gather(1)
    next(g1)

    offset = me * shard
    step = 256
    loads[4].wait()
    top = jnp.full((1, tokens), -jnp.inf, F32)
    for k in range(3):
        land(0, k)
        lo, span = sets[k]
        h = x_all[g, 0, :, :, lo:lo + span].reshape(tokens, span)
        for i in range(0, shard, step):
            lg = lax.dot_general(table[i:i + step, lo:lo + span], h, (((1,), (1,)), ((), ())),
                                 preferred_element_type=F32)
            if k > 0:
                lg = lg + logits[i:i + step]
            if k == 2:
                top = jnp.maximum(top, jnp.max(lg, axis=0, keepdims=True))
            logits[i:i + step] = lg
    loads[3].wait()
    total = jnp.zeros((1, tokens), F32)
    pick = jnp.zeros((1, tokens), F32)
    tgt = tgt_ref[...]
    for i in range(0, shard, step):
        lg = logits[i:i + step]
        vocab_row = offset + i + lax.broadcasted_iota(jnp.int32, (step, tokens), 0)
        total = total + jnp.sum(jnp.exp(lg - top), axis=0, keepdims=True)
        pick = pick + jnp.sum(jnp.where(vocab_row == tgt, lg, 0.0), axis=0, keepdims=True)
    line = lax.broadcasted_iota(jnp.int32, (4, tokens), 0)
    mine = jnp.where(line == 0, top, jnp.where(line == 1, total, pick))
    st[pl.ds(me, 1)] = mine[None]
    stats = [push(st.at[me], st.at[me], (me + d) % n) for d in range(1, n)]

    next(g1)
    spread(0)
    loads[2].wait()
    for d in range(1, groups):
        late.append(push(ids.at[0], ids.at[groups - d], me, (g + d) % groups))
    next(g1)

    for c in stats:
        c.wait_recv()
    top = st[0, 0:1]
    for j in range(1, n):
        top = jnp.maximum(top, st[j, 0:1])
    total = jnp.zeros((1, tokens), F32)
    pick = jnp.zeros((1, tokens), F32)
    for j in range(n):
        total = total + st[j, 1:2] * jnp.exp(st[j, 0:1] - top)
        pick = pick + st[j, 2:3]
    lse = top + jnp.log(total)
    loss_ref[...] = lse - pick
    for i in range(0, shard, step):
        vocab_row = offset + i + lax.broadcasted_iota(jnp.int32, (step, tokens), 0)
        hit = (vocab_row == tgt).astype(F32)
        d = (jnp.exp(logits[i:i + step] - lse) - hit).astype(BF16)
        dl_ref[i:i + step] = d
        dlt_ref[:, i:i + step] = d.T

    chunks = chunk_list(half)
    firsts, seconds, lasts = {}, {}, []

    def send_first(c):
        lo, wide = chunks[c]
        for side in range(2):
            base = side * half + lo
            p = jnp.dot(dlt_ref[...], table[:, base:base + wide], preferred_element_type=F32)
            part[:, :, :, :, base:base + wide] = p.reshape(nz, 2, 2, rows, wide)
            if side == 0:
                p = part[:, pl.ds(1 - y, 1), :, :, base:base + wide]
            else:
                p = part[:, :, pl.ds(1 - x, 1), :, base:base + wide]
            s1[side, :, :, :, lo:lo + wide] = p.reshape(nz, 2, rows, wide).astype(BF16)
            cols = pl.ds(lo, wide)
            firsts[side, c] = push(s1.at[side, :, :, :, cols], r1.at[side, :, :, :, cols],
                                   y_peer if side == 0 else x_peer)

    def merged_first(side, c, zz, yy, xx, count):
        lo, wide = chunks[c]
        base = side * half + lo
        a = part[pl.ds(zz, count), pl.ds(yy, 1), pl.ds(xx, 1), :, base:base + wide].reshape(count, rows, wide)
        b = r1[side, pl.ds(zz, count), pl.ds(xx if side == 0 else yy, 1), :, lo:lo + wide].reshape(count, rows, wide)
        return a + b.astype(F32)

    def send_second(c):
        lo, wide = chunks[c]
        for side in range(2):
            firsts[side, c].wait_recv()
            yy, xx, peer = (y, 1 - x, x_peer) if side == 0 else (1 - y, x, y_peer)
            s2[side, :, :, lo:lo + wide] = merged_first(side, c, 0, yy, xx, nz).astype(BF16)
            cols = pl.ds(lo, wide)
            seconds[side, c] = push(s2.at[side, :, :, cols], r2.at[side, :, :, cols], peer)

    def merged(side, c, zz):
        lo, wide = chunks[c]
        return (merged_first(side, c, zz, y, x, 1)
                + r2[side, pl.ds(zz, 1), :, lo:lo + wide].astype(F32)).reshape(rows, wide)

    def send_last(c):
        lo, wide = chunks[c]
        for side in range(2):
            seconds[side, c].wait_recv()
            for d in range(1, nz):
                zz = (z + d) % nz
                s3[side, d - 1, :, lo:lo + wide] = merged(side, c, zz).astype(BF16)
                cols = pl.ds(lo, wide)
                lasts.append((c, side, push(s3.at[side, d - 1, :, cols], r3.at[side, d - 1, :, cols], at(zz, y, x))))

    def tail(c):
        lo, wide = chunks[c]
        for side in range(2):
            for cc, ss, q in lasts:
                if (cc, ss) == (c, side):
                    q.wait_recv()
            acc = merged(side, c, z)
            for d in range(1, nz):
                acc = acc + r3[side, d - 1, :, lo:lo + wide].astype(F32)
            base = side * half + lo
            hg_ref[:, base:base + wide] = acc.astype(BF16)

    def send_dl():
        for d in range(1, groups):
            peer = (g + d) % groups
            late.append(push(dl_ref.at[pl.ds(pl.multiple_of(peer * piece, piece), piece)],
                             e_in.at[groups - d - 1], me, peer))

    def build_hot():
        line = me * shard + g * piece + lax.broadcasted_iota(jnp.int32, (piece, tokens), 0)
        for d in range(groups):
            hot[d] = (line == ids[d]).astype(F32).astype(BF16)

    def grad(t):
        cols = slice(t * TILE, (t + 1) * TILE)
        acc = jnp.dot(dl_ref[pl.ds(pl.multiple_of(g * piece, piece), piece)],
                      x_all[g, 0, :, :, cols].reshape(tokens, TILE), preferred_element_type=F32)
        acc = acc + jnp.dot(hot[0], x_all[g, 1, :, :, cols].reshape(tokens, TILE), preferred_element_type=F32)
        for d in range(1, groups):
            gg = (g + d) % groups
            acc = acc + jnp.dot(e_in[d - 1], x_all[gg, 0, :, :, cols].reshape(tokens, TILE),
                                preferred_element_type=F32)
            acc = acc + jnp.dot(hot[d], x_all[gg, 1, :, :, cols].reshape(tokens, TILE),
                                preferred_element_type=F32)
        tg_ref[:, cols] = acc

    tiles = width // TILE
    send_first(0)
    send_first(1)
    send_dl()
    next(g1)
    send_second(0)
    send_first(2)
    for _ in g1:
        pass
    send_second(1)
    send_first(3)
    send_last(0)
    send_second(2)
    for k in range(3):
        land(1, k)
    spread(1)
    send_last(1)
    send_second(3)
    for c in late:
        c.wait_recv()
    build_hot()
    send_last(2)
    for t in range(tiles // 2):
        grad(t)
    send_last(3)
    for t in range(tiles // 2, tiles):
        grad(t)
    for c in range(4):
        tail(c)
    for cond, c in started:
        when(cond, c.wait_send)


def write_kernel(tg_ref, hg_ref, loss_ref, tg_out, hg_out, loss_out, sem):
    width = tg_ref.shape[1]
    parts = tg_ref.shape[0] // 64
    copies = [pltpu.make_async_copy(hg_ref, hg_out, sem.at[0]), pltpu.make_async_copy(loss_ref, loss_out, sem.at[1])]
    for i in range(parts):
        r = pl.ds(i * 64, 64)
        copies.append(pltpu.make_async_copy(tg_ref.at[r], tg_out.at[r], sem.at[2 + i]))
    for c in copies:
        c.start()
    for c in copies:
        c.wait()


def solution(mesh):
    groups, n = mesh.shape["dp"], mesh.shape["vocab"]

    def body(table, hidden, cotangent, input_ids, target_ids):
        rows, width = hidden.shape
        shard = table.shape[0]
        nz = n // 4
        tokens = n * rows
        half = width // 2
        piece = shard // groups
        copies = count_copies(groups, n, len(chunk_list(half)))
        anys = pl.BlockSpec(memory_space=pl.ANY)
        vmem = pl.BlockSpec(memory_space=pltpu.VMEM)
        buffers = [
            pltpu.VMEM((shard, width), BF16),
            pltpu.VMEM((groups, 2, n, rows, width), BF16),
            pltpu.VMEM((shard, tokens), F32),
            pltpu.VMEM((n, 4, tokens), F32),
            pltpu.VMEM((shard, tokens), BF16),
            pltpu.VMEM((tokens, shard), BF16),
            pltpu.VMEM((groups - 1, piece, tokens), BF16),
            pltpu.VMEM((groups, piece, tokens), BF16),
            pltpu.VMEM((groups, 1, tokens), jnp.int32),
            pltpu.VMEM((1, tokens), jnp.int32),
            pltpu.VMEM((nz, 2, 2, rows, width), F32),
            pltpu.VMEM((2, nz, 2, rows, half), BF16),
            pltpu.VMEM((2, nz, 2, rows, half), BF16),
            pltpu.VMEM((2, nz, rows, half), BF16),
            pltpu.VMEM((2, nz, rows, half), BF16),
            pltpu.VMEM((2, nz - 1, rows, half), BF16),
            pltpu.VMEM((2, nz - 1, rows, half), BF16),
        ]
        used = sum(math.prod(b.shape) * jnp.dtype(b.dtype).itemsize for b in buffers)
        tg, hg, loss = pl.pallas_call(
            functools.partial(kernel, groups, n),
            out_shape=(
                pltpu.VMEM((piece, width), F32),
                pltpu.VMEM((rows, width), BF16),
                pltpu.VMEM((1, tokens), F32),
            ),
            in_specs=[anys] * 5,
            out_specs=(vmem, vmem, vmem),
            scratch_shapes=buffers + [
                pltpu.SemaphoreType.DMA((5,)),
                pltpu.SemaphoreType.DMA((copies,)),
                pltpu.SemaphoreType.DMA((copies,)),
            ],
            compiler_params=pltpu.CompilerParams(
                collective_id=0, has_side_effects=True, vmem_limit_bytes=used + 6 * 2**20),
        )(*(pltpu.with_memory_space_constraint(a, pltpu.HBM) for a in (
            table, hidden, cotangent, input_ids.reshape(1, tokens), target_ids.reshape(1, tokens))))
        tg = pltpu.with_memory_space_constraint(tg, pltpu.VMEM)
        hg = pltpu.with_memory_space_constraint(hg, pltpu.VMEM)
        loss = pltpu.with_memory_space_constraint(loss, pltpu.VMEM)
        table_grad, hg, loss = pl.pallas_call(
            write_kernel,
            out_shape=(
                jax.ShapeDtypeStruct((piece, width), F32),
                jax.ShapeDtypeStruct((rows, width), BF16),
                jax.ShapeDtypeStruct((1, tokens), F32),
            ),
            in_specs=[vmem] * 3,
            out_specs=(anys,) * 3,
            scratch_shapes=[pltpu.SemaphoreType.DMA((2 + piece // 64,))],
            compiler_params=pltpu.CompilerParams(vmem_limit_bytes=2 * 2**20),
        )(tg, hg, loss)
        return table_grad, hg, loss.reshape(tokens)

    return jax.shard_map(
        body,
        mesh=mesh,
        in_specs=(
            P("vocab", None),
            P(("dp", "vocab"), None),
            P(("dp", "vocab"), None),
            P("dp"),
            P("dp"),
        ),
        out_specs=(P(("vocab", "dp"), None), P(("dp", "vocab"), None), P("dp")),
        check_vma=False,
    )
```

time: 85.8 us -> 72.4 us (0.84)
  Pallas kernels: 83.6 us -> 71.6 us
  local copies, waits for them, and re-layouts: 1.23 us -> 0 us
    pallas_call x2, Pallas kernels: 83.6 us -> 71.6 us  [the longest x1 68.2 us: body(): pl.pallas_call(functools.partial(kernel, groups, n), out_shape=(pltpu.VME...]
    unnamed x6 -> x0, local copies, waits for them, and re-layouts: 1.23 us -> none
where the time goes in v1:
time: 72.4 us; the launch traced here: 72.3 us
  Pallas kernels  71.6 us (99%)
    pallas_call x1, Pallas kernels, body(): pl.pallas_call(functools.partial(kernel, groups, n), out_shape=(pltpu.VME...  68.2 us
    pallas_call x1, Pallas kernels, body(): pl.pallas_call(write_kernel, out_shape=(jax.ShapeDtypeStruct((piece, widt...  3.43 us

profile of v1, /device:TPU:0, one launch (start us, length us, event | category | flops | bytes accessed | tf_op | source)
XLA Modules:
  0.0 72.3 jit_solution(8374269897840486764)
XLA Ops:
  0.6 68.2 %shard_map.76 = (f32[512,4096]{1,0:T(8,128)S(1)}, bf16[16,4096]{1,0:T(8,128)(2,1)S(1)}, f32[1,256]{1,0:T(1,128)S(1)}) custom-call(bf16[1024,4096]{1,0:T(8,128)(2,1)} %table_hbm.1, bf16[16,4096]{1,0:T(8,128)(2,1)} %hidden_hbm.1, bf16[16,4096]{1,0:T(8,128)(2,1)} %cot_hbm.1, s32[1,256]{1,0:T(1,128)} %bitcast.3, s32[1,256]{1,0:T(1,128)} %bitcast.4), custom_call_target="tpu_custom_call" | custom-call | tf_op jit(solution)/shard_map/pallas_call | solution.py:410
  68.8 3.4 %shard_map.77 = (f32[512,4096]{1,0:T(8,128)}, bf16[16,4096]{1,0:T(8,128)(2,1)}, f32[1,256]{1,0:T(1,128)}) custom-call(f32[512,4096]{1,0:T(8,128)S(1)} %get-tuple-element.9.tg_ref, bf16[16,4096]{1,0:T(8,128)(2,1)S(1)} %get-tuple-element.10.hg_ref, f32[1,256]{1,0:T(1,128)S(1)} %get-tuple-element.11.loss_ref), custom_call_target="tpu_custom_call" | custom-call | tf_op jit(solution)/shard_map/pallas_call | solution.py:431

commit v2 on v1

v2 whole, which is shorter than its diff:
```python
import functools
import math

import jax
import jax.numpy as jnp
from jax import lax
from jax.experimental import pallas as pl
from jax.experimental.pallas import tpu as pltpu
from jax.sharding import PartitionSpec as P

MESH = pl.DeviceIdType.MESH
BF16 = jnp.bfloat16
F32 = jnp.float32
TILE = 512
HIDDEN_A = 6
COT_A = 6


def chunk_list(half):
    eighth = half // 8
    spans, lo = [], 0
    for k in (2, 3, 2, 1):
        spans.append((lo, k * eighth))
        lo += k * eighth
    return spans


def count_semaphores(groups, n, chunks):
    nz = n // 4
    gather = 2 + 7 * nz + 3
    return 12 + 1 + 3 + 4 * (groups - 1), 2 * gather + 1 + 6 * chunks + 4 * (groups - 1)


def kernel(groups, n, table_hbm, hidden_hbm, cot_hbm, in_ids_hbm, tgt_hbm,
           tg_ref, hg_ref, loss_ref,
           table, x_all, logits, st, dl_ref, dlt_ref, e_in, hot, ids, tgt_ref,
           part, s1, r1, s2, r2, s3, r3, load_sem, send, recv):
    nz = n // 4
    rows, width = hg_ref.shape
    shard = table.shape[0]
    tokens = n * rows
    piece = shard // groups
    half = width // 2
    me = lax.axis_index("vocab")
    g = lax.axis_index("dp")
    z = me // 4
    y = (me % 4) // 2
    x = me % 2
    send_slots, recv_slots = iter(range(send.shape[0])), iter(range(recv.shape[0]))

    def at(zz, yy, xx):
        return zz * 4 + yy * 2 + xx

    x_peer = at(z, y, 1 - x)
    y_peer = at(z, 1 - y, x)
    above, below = z + 1 < nz, z > 0
    up, down = at(jnp.minimum(z + 1, nz - 1), y, x), at(jnp.maximum(z - 1, 0), y, x)

    def when(cond, act):
        if cond is None:
            act()
        else:
            pl.when(cond)(act)

    def every(cond, acts):
        def act():
            for one in acts:
                one()
        when(cond, act)

    barrier = pltpu.get_barrier_semaphore()

    def greet(v, gg=None):
        pl.semaphore_signal(barrier, inc=1, device_id=(g if gg is None else gg, v), device_id_type=MESH)

    greet(x_peer)
    greet(y_peer)
    when(above, lambda: greet(up))
    when(below, lambda: greet(down))
    for d in range(1, groups):
        greet(me, (g + d) % groups)

    loads = [
        pltpu.make_async_copy(hidden_hbm, x_all.at[g, 0, me], load_sem.at[0]),
        pltpu.make_async_copy(cot_hbm, x_all.at[g, 1, me], load_sem.at[1]),
        pltpu.make_async_copy(in_ids_hbm, ids.at[0], load_sem.at[2]),
        pltpu.make_async_copy(tgt_hbm, tgt_ref, load_sem.at[3]),
        pltpu.make_async_copy(table_hbm, table, load_sem.at[4]),
    ]
    for c in loads:
        c.start()
    loads[0].wait()
    pl.semaphore_wait(barrier, 2 + above.astype(jnp.int32) + below.astype(jnp.int32) + groups - 1)

    owed = []

    def push(src, dst, v, out, into, gg=None, cond=None, start=True):
        c = pltpu.make_async_remote_copy(
            src_ref=src, dst_ref=dst, send_sem=send.at[out], recv_sem=recv.at[into],
            device_id=(g if gg is None else gg, v), device_id_type=MESH)
        if start:
            when(cond, c.start)
        return c

    def drain():
        for cond, ref, out in owed:
            c = pltpu.make_async_remote_copy(
                src_ref=ref, dst_ref=ref, send_sem=send.at[out], recv_sem=recv.at[0],
                device_id=(g, me), device_id_type=MESH)
            when(cond, c.wait_send)
        owed.clear()

    def arrive(ref, into):
        pltpu.make_async_remote_copy(
            src_ref=ref, dst_ref=ref, send_sem=send.at[0], recv_sem=recv.at[into],
            device_id=(g, me), device_id_type=MESH).wait_recv()

    def take(it, count):
        return [next(it) for _ in range(count)][0]

    def split(k):
        wa = width * k // 16
        wb = (width - wa) // 2
        return [(0, wa), (wa, wb), (wa + wb, wb)]

    both = [split(HIDDEN_A), split(COT_A)]
    sets = both[0]
    inner = jnp.logical_and(above, below)
    outer = jnp.logical_not(inner)
    ways = []
    for s in range(nz - 1):
        lower, upper = z - 1 - s >= 0, z + 1 + s < nz
        ways.append(((lower, jnp.maximum(z - 1 - s, 0), above, up), (upper, jnp.minimum(z + 1 + s, nz - 1), below, down)))

    class Gather:
        def __init__(self, kind):
            self.kind, self.sets = kind, both[kind]
            self.swap_out, self.fan_a, self.fan_bc = (next(send_slots) for _ in range(3))
            self.line_out = [next(send_slots) for _ in range(3)]
            self.swap_in = [None, next(recv_slots), next(recv_slots)]
            self.full = [next(recv_slots) for _ in range(3)]
            self.via = {0: take(recv_slots, nz), 1: take(recv_slots, nz)}

            def some(k, count):
                return x_all.at[g, kind, pl.ds(0, count), :, pl.ds(*self.sets[k])]

            self.some = some
            self.columns = {}

        def owe(self):
            owed.append((None, self.some(1, 1), self.swap_out))
            owed.append((None, self.some(2, 1), self.swap_out))
            owed.append((None, self.some(0, 3 * nz), self.fan_a))
            owed.append((None, self.some(1, 2 * nz), self.fan_bc))
            owed.append((None, self.some(2, 2 * nz), self.fan_bc))
            for k in range(3):
                lines = 1 if k == 0 else 2
                owed.append((inner, self.some(k, lines * (nz + 1)), self.line_out[k]))
                owed.append((outer, self.some(k, lines), self.line_out[k]))

        def blk(self, k, zz, yy, xx):
            return x_all.at[g, self.kind, at(zz, yy, xx), :, pl.ds(*self.sets[k])]

        def swap(self):
            for k, peer in ((1, x_peer), (2, y_peer)):
                b = self.blk(k, z, y, x)
                push(b, b, peer, self.swap_out, self.swap_in[k])

        def line(self, name, k, yy, xx):
            base = take(recv_slots, nz)
            self.columns[name] = (k, yy, xx, base)
            b = self.blk(k, z, yy, xx)
            push(b, b, up, self.line_out[k], base + z, cond=above)
            push(b, b, down, self.line_out[k], base + z, cond=below)

        def lines1(self):
            self.line("a", 0, y, x)
            self.line("b1", 1, y, x)
            self.line("c1", 2, y, x)

        def lines2(self):
            arrive(self.blk(1, z, y, x), self.swap_in[1])
            self.line("b2", 1, y, 1 - x)
            arrive(self.blk(2, z, y, x), self.swap_in[2])
            self.line("c2", 2, 1 - y, x)

        def fans(self, name, zz):
            k, yy, xx, _ = self.columns[name]
            b = self.blk(k, zz, yy, xx)
            if k == 0:
                return [push(b, b, x_peer, self.fan_a, self.via[0] + zz, start=False),
                        push(b, b, y_peer, self.fan_a, self.via[1] + zz, start=False)]
            return [push(b, b, y_peer if k == 1 else x_peer, self.fan_bc, self.full[k], start=False)]

        def share(self, *names):
            for name in names:
                for c in self.fans(name, z):
                    c.start()

        def step(self, s, *names):
            for name in names:
                k, yy, xx, base = self.columns[name]
                for cond, zz, go, nxt in ways[s]:
                    b = self.blk(k, zz, yy, xx)
                    relay = push(b, b, nxt, self.line_out[k], base + zz, start=False)
                    fans = self.fans(name, zz)

                    def act():
                        relay.wait_recv()
                        if s < nz - 2:
                            pl.when(go)(relay.start)
                        for c in fans:
                            c.start()

                    pl.when(cond)(act)

        def third(self, s):
            lo, span = self.sets[0]
            for cond, zz in [(None, z)] if s < 0 else [(w[0], w[1]) for w in ways[s]]:
                full = self.blk(0, zz, y, x)
                b = x_all.at[g, self.kind, at(zz, y, 1 - x), :, pl.ds(lo, span // 2)]
                tx = push(b, b, y_peer, self.fan_a, self.full[0], start=False)
                b = x_all.at[g, self.kind, at(zz, 1 - y, x), :, pl.ds(lo + span // 2, span // 2)]
                ty = push(b, b, x_peer, self.fan_a, self.full[0], start=False)

                def act():
                    arrive(full, self.via[0] + zz)
                    tx.start()
                    arrive(full, self.via[1] + zz)
                    ty.start()

                when(cond, act)

        def land(self, k):
            arrive(self.some(k, nz if k == 0 else 2 * nz), self.full[k])

    late = []

    def lone(src, dst, gg):
        k = next(send_slots)
        owed.append((None, src, k))
        return push(src, dst, me, k, next(recv_slots), gg)

    def spread(kind):
        for d in range(1, groups):
            late.append(lone(x_all.at[g, kind], x_all.at[g, kind], (g + d) % groups))

    g0, g1 = Gather(0), Gather(1)
    g0.swap()
    g0.lines1()
    g0.share("a", "b1", "c1")
    g0.lines2()
    g0.share("b2", "c2")
    loads[1].wait()
    g1.swap()
    for s in range(nz - 2):
        g0.step(s, "a")
        g0.third(s - 1)
        g0.step(s, "b1", "c1", "b2", "c2")
    g1.lines1()
    g1.lines2()
    g0.step(nz - 2, "a")
    g0.third(nz - 3)
    g0.step(nz - 2, "b1", "c1")
    g0.third(nz - 2)
    g0.step(nz - 2, "b2", "c2")
    g0.owe()
    g1.share("a", "b1", "c1", "b2", "c2")

    offset = me * shard
    step = 256
    loads[4].wait()
    top = jnp.full((1, tokens), -jnp.inf, F32)
    for k in range(3):
        with jax.named_scope('land'):
            g0.land(k)
        lo, span = sets[k]
        h = x_all[g, 0, :, :, lo:lo + span].reshape(tokens, span)
        for i in range(0, shard, step):
            lg = lax.dot_general(table[i:i + step, lo:lo + span], h, (((1,), (1,)), ((), ())),
                                 preferred_element_type=F32)
            if k > 0:
                lg = lg + logits[i:i + step]
            if k == 2:
                top = jnp.maximum(top, jnp.max(lg, axis=0, keepdims=True))
            logits[i:i + step] = lg
    g1.step(0, "a")
    g1.third(-1)
    g1.step(0, "b1", "c1", "b2", "c2")
    loads[3].wait()
    total = jnp.zeros((1, tokens), F32)
    pick = jnp.zeros((1, tokens), F32)
    tgt = tgt_ref[...]
    for i in range(0, shard, step):
        lg = logits[i:i + step]
        vocab_row = offset + i + lax.broadcasted_iota(jnp.int32, (step, tokens), 0)
        total = total + jnp.sum(jnp.exp(lg - top), axis=0, keepdims=True)
        pick = pick + jnp.sum(jnp.where(vocab_row == tgt, lg, 0.0), axis=0, keepdims=True)
    line = lax.broadcasted_iota(jnp.int32, (4, tokens), 0)
    mine = jnp.where(line == 0, top, jnp.where(line == 1, total, pick))
    st[pl.ds(me, 1)] = mine[None]
    stat_out, stat_in = next(send_slots), next(recv_slots)
    for d in range(1, n):
        push(st.at[me], st.at[me], (me + d) % n, stat_out, stat_in)
    owed.append((None, st.at[pl.ds(0, n - 1)], stat_out))

    spread(0)
    loads[2].wait()
    for d in range(1, groups):
        late.append(lone(ids.at[0], ids.at[groups - d], (g + d) % groups))
    for s in range(1, nz - 2):
        g1.step(s, "a")
        g1.third(s - 1)
        g1.step(s, "b1", "c1", "b2", "c2")
    arrive(st.at[pl.ds(0, n - 1)], stat_in)
    top = st[0, 0:1]
    for j in range(1, n):
        top = jnp.maximum(top, st[j, 0:1])
    total = jnp.zeros((1, tokens), F32)
    pick = jnp.zeros((1, tokens), F32)
    for j in range(n):
        total = total + st[j, 1:2] * jnp.exp(st[j, 0:1] - top)
        pick = pick + st[j, 2:3]
    lse = top + jnp.log(total)
    loss_ref[...] = lse - pick
    for i in range(0, shard, step):
        vocab_row = offset + i + lax.broadcasted_iota(jnp.int32, (step, tokens), 0)
        hit = (vocab_row == tgt).astype(F32)
        d = (jnp.exp(logits[i:i + step] - lse) - hit).astype(BF16)
        dl_ref[i:i + step] = d
        dlt_ref[:, i:i + step] = d.T

    chunks = chunk_list(half)
    outs = [next(send_slots) for _ in range(3)]
    owed.extend([(None, s1, outs[0]), (None, s2, outs[1]), (None, s3, outs[2])])
    ins = {(stage, side, c): next(recv_slots) for stage in range(3) for side in range(2) for c in range(len(chunks))}

    def send_first(c):
        lo, wide = chunks[c]
        for side in range(2):
            base = side * half + lo
            p = jnp.dot(dlt_ref[...], table[:, base:base + wide], preferred_element_type=F32)
            part[:, :, :, :, base:base + wide] = p.reshape(nz, 2, 2, rows, wide)
            if side == 0:
                p = part[:, pl.ds(1 - y, 1), :, :, base:base + wide]
            else:
                p = part[:, :, pl.ds(1 - x, 1), :, base:base + wide]
            s1[side, :, :, :, lo:lo + wide] = p.reshape(nz, 2, rows, wide).astype(BF16)
            cols = pl.ds(lo, wide)
            push(s1.at[side, :, :, :, cols], r1.at[side, :, :, :, cols],
                 y_peer if side == 0 else x_peer, outs[0], ins[0, side, c])

    def merged_first(side, c, zz, yy, xx, count):
        lo, wide = chunks[c]
        base = side * half + lo
        a = part[pl.ds(zz, count), pl.ds(yy, 1), pl.ds(xx, 1), :, base:base + wide].reshape(count, rows, wide)
        b = r1[side, pl.ds(zz, count), pl.ds(xx if side == 0 else yy, 1), :, lo:lo + wide].reshape(count, rows, wide)
        return a + b.astype(F32)

    def send_second(c):
        lo, wide = chunks[c]
        for side in range(2):
            arrive(r1.at[side, :, :, :, pl.ds(lo, wide)], ins[0, side, c])
            yy, xx, peer = (y, 1 - x, x_peer) if side == 0 else (1 - y, x, y_peer)
            s2[side, :, :, lo:lo + wide] = merged_first(side, c, 0, yy, xx, nz).astype(BF16)
            cols = pl.ds(lo, wide)
            push(s2.at[side, :, :, cols], r2.at[side, :, :, cols], peer, outs[1], ins[1, side, c])

    def merged(side, c, zz):
        lo, wide = chunks[c]
        return (merged_first(side, c, zz, y, x, 1)
                + r2[side, pl.ds(zz, 1), :, lo:lo + wide].astype(F32)).reshape(rows, wide)

    def send_last(c):
        lo, wide = chunks[c]
        for side in range(2):
            arrive(r2.at[side, :, :, pl.ds(lo, wide)], ins[1, side, c])
            for d in range(1, nz):
                zz = (z + d) % nz
                s3[side, d - 1, :, lo:lo + wide] = merged(side, c, zz).astype(BF16)
                cols = pl.ds(lo, wide)
                push(s3.at[side, d - 1, :, cols], r3.at[side, d - 1, :, cols], at(zz, y, x), outs[2], ins[2, side, c])

    def tail(c):
        lo, wide = chunks[c]
        for side in range(2):
            arrive(r3.at[side, :, :, pl.ds(lo, wide)], ins[2, side, c])
            acc = merged(side, c, z)
            for d in range(1, nz):
                acc = acc + r3[side, d - 1, :, lo:lo + wide].astype(F32)
            base = side * half + lo
            hg_ref[:, base:base + wide] = acc.astype(BF16)

    def send_dl():
        for d in range(1, groups):
            peer = (g + d) % groups
            late.append(lone(dl_ref.at[pl.ds(pl.multiple_of(peer * piece, piece), piece)],
                             e_in.at[groups - d - 1], peer))

    def build_hot():
        line = me * shard + g * piece + lax.broadcasted_iota(jnp.int32, (piece, tokens), 0)
        for d in range(groups):
            hot[d] = (line == ids[d]).astype(F32).astype(BF16)

    def settle():
        for c in late:
            c.wait_recv()
        late.clear()

    def grad(t, kind):
        cols = slice(t * TILE, (t + 1) * TILE)
        acc = None
        for d in range(groups):
            if kind == 1:
                e = hot[d]
            elif d == 0:
                e = dl_ref[pl.ds(pl.multiple_of(g * piece, piece), piece)]
            else:
                e = e_in[d - 1]
            p = jnp.dot(e, x_all[(g + d) % groups, kind, :, :, cols].reshape(tokens, TILE),
                        preferred_element_type=F32)
            acc = p if acc is None else acc + p
        if kind == 1:
            acc = acc + tg_ref[:, cols]
        tg_ref[:, cols] = acc

    tiles = width // TILE
    send_first(0)
    send_dl()
    send_first(1)
    settle()
    build_hot()
    for t in range(tiles):
        grad(t, 0)
    g1.step(nz - 2, "a")
    g1.third(nz - 3)
    g1.step(nz - 2, "b1", "c1")
    g1.third(nz - 2)
    g1.step(nz - 2, "b2", "c2")
    g1.owe()
    send_second(0)
    send_first(2)
    send_second(1)
    send_last(0)
    send_first(3)
    for k in range(3):
        g1.land(k)
    spread(1)
    send_second(2)
    send_last(1)
    send_second(3)
    send_last(2)
    send_last(3)
    settle()
    for t in range(tiles):
        grad(t, 1)
    drain()
    for c in range(len(chunks)):
        tail(c)


def write_kernel(tg_ref, hg_ref, loss_ref, tg_out, hg_out, loss_out, sem):
    width = tg_ref.shape[1]
    parts = tg_ref.shape[0] // 64
    copies = [pltpu.make_async_copy(hg_ref, hg_out, sem.at[0]), pltpu.make_async_copy(loss_ref, loss_out, sem.at[1])]
    for i in range(parts):
        r = pl.ds(i * 64, 64)
        copies.append(pltpu.make_async_copy(tg_ref.at[r], tg_out.at[r], sem.at[2 + i]))
    for c in copies:
        c.start()
    for c in copies:
        c.wait()


def solution(mesh):
    groups, n = mesh.shape["dp"], mesh.shape["vocab"]

    def body(table, hidden, cotangent, input_ids, target_ids):
        rows, width = hidden.shape
        shard = table.shape[0]
        nz = n // 4
        tokens = n * rows
        half = width // 2
        piece = shard // groups
        sends, recvs = count_semaphores(groups, n, len(chunk_list(half)))
        anys = pl.BlockSpec(memory_space=pl.ANY)
        vmem = pl.BlockSpec(memory_space=pltpu.VMEM)
        buffers = [
            pltpu.VMEM((shard, width), BF16),
            pltpu.VMEM((groups, 2, n, rows, width), BF16),
            pltpu.VMEM((shard, tokens), F32),
            pltpu.VMEM((n, 4, tokens), F32),
            pltpu.VMEM((shard, tokens), BF16),
            pltpu.VMEM((tokens, shard), BF16),
            pltpu.VMEM((groups - 1, piece, tokens), BF16),
            pltpu.VMEM((groups, piece, tokens), BF16),
            pltpu.VMEM((groups, 1, tokens), jnp.int32),
            pltpu.VMEM((1, tokens), jnp.int32),
            pltpu.VMEM((nz, 2, 2, rows, width), F32),
            pltpu.VMEM((2, nz, 2, rows, half), BF16),
            pltpu.VMEM((2, nz, 2, rows, half), BF16),
            pltpu.VMEM((2, nz, rows, half), BF16),
            pltpu.VMEM((2, nz, rows, half), BF16),
            pltpu.VMEM((2, nz - 1, rows, half), BF16),
            pltpu.VMEM((2, nz - 1, rows, half), BF16),
        ]
        used = sum(math.prod(b.shape) * jnp.dtype(b.dtype).itemsize for b in buffers)
        tg, hg, loss = pl.pallas_call(
            functools.partial(kernel, groups, n),
            out_shape=(
                pltpu.VMEM((piece, width), F32),
                pltpu.VMEM((rows, width), BF16),
                pltpu.VMEM((1, tokens), F32),
            ),
            in_specs=[anys] * 5,
            out_specs=(vmem, vmem, vmem),
            scratch_shapes=buffers + [
                pltpu.SemaphoreType.DMA((5,)),
                pltpu.SemaphoreType.DMA((sends,)),
                pltpu.SemaphoreType.DMA((recvs,)),
            ],
            compiler_params=pltpu.CompilerParams(
                collective_id=0, has_side_effects=True, vmem_limit_bytes=used + 6 * 2**20),
        )(*(pltpu.with_memory_space_constraint(a, pltpu.HBM) for a in (
            table, hidden, cotangent, input_ids.reshape(1, tokens), target_ids.reshape(1, tokens))))
        tg = pltpu.with_memory_space_constraint(tg, pltpu.VMEM)
        hg = pltpu.with_memory_space_constraint(hg, pltpu.VMEM)
        loss = pltpu.with_memory_space_constraint(loss, pltpu.VMEM)
        table_grad, hg, loss = pl.pallas_call(
            write_kernel,
            out_shape=(
                jax.ShapeDtypeStruct((piece, width), F32),
                jax.ShapeDtypeStruct((rows, width), BF16),
                jax.ShapeDtypeStruct((1, tokens), F32),
            ),
            in_specs=[vmem] * 3,
            out_specs=(anys,) * 3,
            scratch_shapes=[pltpu.SemaphoreType.DMA((2 + piece // 64,))],
            compiler_params=pltpu.CompilerParams(vmem_limit_bytes=2 * 2**20),
        )(tg, hg, loss)
        return table_grad, hg, loss.reshape(tokens)

    return jax.shard_map(
        body,
        mesh=mesh,
        in_specs=(
            P("vocab", None),
            P(("dp", "vocab"), None),
            P(("dp", "vocab"), None),
            P("dp"),
            P("dp"),
        ),
        out_specs=(P(("vocab", "dp"), None), P(("dp", "vocab"), None), P("dp")),
        check_vma=False,
    )
```

time: 72.4 us -> 66.1 us (0.913)
  Pallas kernels: 71.6 us -> 65.4 us
    pallas_call x1, Pallas kernels: 68.2 us -> 61.9 us  [body(): pl.pallas_call(functools.partial(kernel, groups, n), out_shape=(pltpu.VME...]
where the time goes in v2:
time: 66.1 us; the launch traced here: 66 us
  Pallas kernels  65.4 us (99%)
    pallas_call x1, Pallas kernels, body(): pl.pallas_call(functools.partial(kernel, groups, n), out_shape=(pltpu.VME...  61.9 us
    pallas_call x1, Pallas kernels, body(): pl.pallas_call(write_kernel, out_shape=(jax.ShapeDtypeStruct((piece, widt...  3.43 us

profile of v2, /device:TPU:0, one launch (start us, length us, event | category | flops | bytes accessed | tf_op | source)
XLA Modules:
  0.0 66.0 jit_solution(9358485404943589851)
XLA Ops:
  0.6 61.9 %shard_map.76 = (f32[512,4096]{1,0:T(8,128)S(1)}, bf16[16,4096]{1,0:T(8,128)(2,1)S(1)}, f32[1,256]{1,0:T(1,128)S(1)}) custom-call(bf16[1024,4096]{1,0:T(8,128)(2,1)} %table_hbm.1, bf16[16,4096]{1,0:T(8,128)(2,1)} %hidden_hbm.1, bf16[16,4096]{1,0:T(8,128)(2,1)} %cot_hbm.1, s32[1,256]{1,0:T(1,128)} %bitcast.3, s32[1,256]{1,0:T(1,128)} %bitcast.4), custom_call_target="tpu_custom_call" | custom-call | tf_op jit(solution)/shard_map/pallas_call | solution.py:508
  62.6 3.4 %shard_map.77 = (f32[512,4096]{1,0:T(8,128)}, bf16[16,4096]{1,0:T(8,128)(2,1)}, f32[1,256]{1,0:T(1,128)}) custom-call(f32[512,4096]{1,0:T(8,128)S(1)} %get-tuple-element.9.tg_ref, bf16[16,4096]{1,0:T(8,128)(2,1)S(1)} %get-tuple-element.10.hg_ref, f32[1,256]{1,0:T(1,128)S(1)} %get-tuple-element.11.loss_ref), custom_call_target="tpu_custom_call" | custom-call | tf_op jit(solution)/shard_map/pallas_call | solution.py:529

commit v3 on v2

--- a/solution.py
+++ b/solution.py
@@ -166,23 +166,27 @@
                 b = self.blk(k, z, y, x)
                 push(b, b, peer, self.swap_out, self.swap_in[k])
 
-        def line(self, name, k, yy, xx):
-            base = take(recv_slots, nz)
-            self.columns[name] = (k, yy, xx, base)
+        def register(self):
+            for name, k, yy, xx in (("a", 0, y, x), ("b1", 1, y, x), ("c1", 2, y, x),
+                                    ("b2", 1, y, 1 - x), ("c2", 2, 1 - y, x)):
+                self.columns[name] = (k, yy, xx, take(recv_slots, nz))
+
+        def line(self, name):
+            k, yy, xx, base = self.columns[name]
             b = self.blk(k, z, yy, xx)
             push(b, b, up, self.line_out[k], base + z, cond=above)
             push(b, b, down, self.line_out[k], base + z, cond=below)
 
         def lines1(self):
-            self.line("a", 0, y, x)
-            self.line("b1", 1, y, x)
-            self.line("c1", 2, y, x)
+            self.line("a")
+            self.line("b1")
+            self.line("c1")
 
         def lines2(self):
             arrive(self.blk(1, z, y, x), self.swap_in[1])
-            self.line("b2", 1, y, 1 - x)
+            self.line("b2")
             arrive(self.blk(2, z, y, x), self.swap_in[2])
-            self.line("c2", 2, 1 - y, x)
+            self.line("c2")
 
         def fans(self, name, zz):
             k, yy, xx, _ = self.columns[name]
@@ -245,7 +249,16 @@
         for d in range(1, groups):
             late.append(lone(x_all.at[g, kind], x_all.at[g, kind], (g + d) % groups))
 
+    def lines():
+        g1.lines1()
+        g1.lines2()
+
+    def share():
+        g1.share("a", "b1", "c1", "b2", "c2")
+
     g0, g1 = Gather(0), Gather(1)
+    g0.register()
+    g1.register()
     g0.swap()
     g0.lines1()
     g0.share("a", "b1", "c1")
@@ -257,23 +270,21 @@
         g0.step(s, "a")
         g0.third(s - 1)
         g0.step(s, "b1", "c1", "b2", "c2")
-    g1.lines1()
-    g1.lines2()
     g0.step(nz - 2, "a")
     g0.third(nz - 3)
     g0.step(nz - 2, "b1", "c1")
     g0.third(nz - 2)
     g0.step(nz - 2, "b2", "c2")
     g0.owe()
-    g1.share("a", "b1", "c1", "b2", "c2")
+    lines()
+    share()
 
     offset = me * shard
     step = 256
     loads[4].wait()
     top = jnp.full((1, tokens), -jnp.inf, F32)
     for k in range(3):
-        with jax.named_scope('land'):
-            g0.land(k)
+        g0.land(k)
         lo, span = sets[k]
         h = x_all[g, 0, :, :, lo:lo + span].reshape(tokens, span)
         for i in range(0, shard, step):
@@ -284,9 +295,6 @@
             if k == 2:
                 top = jnp.maximum(top, jnp.max(lg, axis=0, keepdims=True))
             logits[i:i + step] = lg
-    g1.step(0, "a")
-    g1.third(-1)
-    g1.step(0, "b1", "c1", "b2", "c2")
     loads[3].wait()
     total = jnp.zeros((1, tokens), F32)
     pick = jnp.zeros((1, tokens), F32)
@@ -304,6 +312,9 @@
         push(st.at[me], st.at[me], (me + d) % n, stat_out, stat_in)
     owed.append((None, st.at[pl.ds(0, n - 1)], stat_out))
 
+    g1.step(0, "a")
+    g1.third(-1)
+    g1.step(0, "b1", "c1", "b2", "c2")
     spread(0)
     loads[2].wait()
     for d in range(1, groups):
@@ -427,19 +438,17 @@
     tiles = width // TILE
     send_first(0)
     send_dl()
+    g1.step(nz - 2, "a", "b1", "c1", "b2", "c2")
     send_first(1)
     settle()
     build_hot()
     for t in range(tiles):
         grad(t, 0)
-    g1.step(nz - 2, "a")
-    g1.third(nz - 3)
-    g1.step(nz - 2, "b1", "c1")
-    g1.third(nz - 2)
-    g1.step(nz - 2, "b2", "c2")
-    g1.owe()
     send_second(0)
     send_first(2)
+    g1.third(nz - 3)
+    g1.third(nz - 2)
+    g1.owe()
     send_second(1)
     send_last(0)
     send_first(3)

time: 66.1 us -> 65.5 us (level)
  Pallas kernels: 65.4 us -> 64.7 us
where the time goes in v3:
time: 65.5 us; the launch traced here: 65.4 us
  Pallas kernels  64.7 us (99%)
    pallas_call x1, Pallas kernels, body(): pl.pallas_call(functools.partial(kernel, groups, n), out_shape=(pltpu.VME...  61.3 us
    pallas_call x1, Pallas kernels, body(): pl.pallas_call(write_kernel, out_shape=(jax.ShapeDtypeStruct((piece, widt...  3.43 us

profile of v3, /device:TPU:0, one launch (start us, length us, event | category | flops | bytes accessed | tf_op | source)
XLA Modules:
  0.0 65.4 jit_solution(16890864617788769112)
XLA Ops:
  0.6 61.3 %shard_map.76 = (f32[512,4096]{1,0:T(8,128)S(1)}, bf16[16,4096]{1,0:T(8,128)(2,1)S(1)}, f32[1,256]{1,0:T(1,128)S(1)}) custom-call(bf16[1024,4096]{1,0:T(8,128)(2,1)} %table_hbm.1, bf16[16,4096]{1,0:T(8,128)(2,1)} %hidden_hbm.1, bf16[16,4096]{1,0:T(8,128)(2,1)} %cot_hbm.1, s32[1,256]{1,0:T(1,128)} %bitcast.3, s32[1,256]{1,0:T(1,128)} %bitcast.4), custom_call_target="tpu_custom_call" | custom-call | tf_op jit(solution)/shard_map/pallas_call | solution.py:517
  61.9 3.4 %shard_map.77 = (f32[512,4096]{1,0:T(8,128)}, bf16[16,4096]{1,0:T(8,128)(2,1)}, f32[1,256]{1,0:T(1,128)}) custom-call(f32[512,4096]{1,0:T(8,128)S(1)} %get-tuple-element.9.tg_ref, bf16[16,4096]{1,0:T(8,128)(2,1)S(1)} %get-tuple-element.10.hg_ref, f32[1,256]{1,0:T(1,128)S(1)} %get-tuple-element.11.loss_ref), custom_call_target="tpu_custom_call" | custom-call | tf_op jit(solution)/shard_map/pallas_call | solution.py:538

commit v4 on v3

--- a/solution.py
+++ b/solution.py
@@ -27,8 +27,8 @@
 
 def count_semaphores(groups, n, chunks):
     nz = n // 4
-    gather = 2 + 7 * nz + 3
-    return 12 + 1 + 3 + 4 * (groups - 1), 2 * gather + 1 + 6 * chunks + 4 * (groups - 1)
+    gather = 2 + 5 * (nz - 1) + 2 * nz + 3
+    return 12 + 1 + 3 + 4 * (groups - 1), 2 * gather + 1 + 5 * chunks + 4 * (groups - 1)
 
 
 def kernel(groups, n, table_hbm, hidden_hbm, cot_hbm, in_ids_hbm, tgt_hbm,
@@ -169,13 +169,13 @@
         def register(self):
             for name, k, yy, xx in (("a", 0, y, x), ("b1", 1, y, x), ("c1", 2, y, x),
                                     ("b2", 1, y, 1 - x), ("c2", 2, 1 - y, x)):
-                self.columns[name] = (k, yy, xx, take(recv_slots, nz))
+                self.columns[name] = (k, yy, xx, take(recv_slots, nz - 1))
 
         def line(self, name):
             k, yy, xx, base = self.columns[name]
             b = self.blk(k, z, yy, xx)
-            push(b, b, up, self.line_out[k], base + z, cond=above)
-            push(b, b, down, self.line_out[k], base + z, cond=below)
+            push(b, b, up, self.line_out[k], base + jnp.minimum(z, nz - 2), cond=above)
+            push(b, b, down, self.line_out[k], base + jnp.maximum(z - 1, 0), cond=below)
 
         def lines1(self):
             self.line("a")
@@ -205,8 +205,9 @@
             for name in names:
                 k, yy, xx, base = self.columns[name]
                 for cond, zz, go, nxt in ways[s]:
+                    slot = base + (zz if nxt is up else zz - 1)
                     b = self.blk(k, zz, yy, xx)
-                    relay = push(b, b, nxt, self.line_out[k], base + zz, start=False)
+                    relay = push(b, b, nxt, self.line_out[k], slot, start=False)
                     fans = self.fans(name, zz)
 
                     def act():
@@ -344,7 +345,8 @@
     chunks = chunk_list(half)
     outs = [next(send_slots) for _ in range(3)]
     owed.extend([(None, s1, outs[0]), (None, s2, outs[1]), (None, s3, outs[2])])
-    ins = {(stage, side, c): next(recv_slots) for stage in range(3) for side in range(2) for c in range(len(chunks))}
+    ins = {(stage, side, c): next(recv_slots) for stage in range(2) for side in range(2) for c in range(len(chunks))}
+    ends = [next(recv_slots) for _ in chunks]
 
     def send_first(c):
         lo, wide = chunks[c]
@@ -390,12 +392,12 @@
                 zz = (z + d) % nz
                 s3[side, d - 1, :, lo:lo + wide] = merged(side, c, zz).astype(BF16)
                 cols = pl.ds(lo, wide)
-                push(s3.at[side, d - 1, :, cols], r3.at[side, d - 1, :, cols], at(zz, y, x), outs[2], ins[2, side, c])
+                push(s3.at[side, d - 1, :, cols], r3.at[side, d - 1, :, cols], at(zz, y, x), outs[2], ends[c])
 
     def tail(c):
         lo, wide = chunks[c]
+        arrive(r3.at[:, :, :, pl.ds(lo, wide)], ends[c])
         for side in range(2):
-            arrive(r3.at[side, :, :, pl.ds(lo, wide)], ins[2, side, c])
             acc = merged(side, c, z)
             for d in range(1, nz):
                 acc = acc + r3[side, d - 1, :, lo:lo + wide].astype(F32)

time: 65.5 us -> 65.4 us (level)
  no operation moved by 1% of the time
where the time goes in v4:
time: 65.4 us; the launch traced here: 65.2 us
  Pallas kernels  64.6 us (99%)
    pallas_call x1, Pallas kernels, body(): pl.pallas_call(functools.partial(kernel, groups, n), out_shape=(pltpu.VME...  61.2 us
    pallas_call x1, Pallas kernels, body(): pl.pallas_call(write_kernel, out_shape=(jax.ShapeDtypeStruct((piece, widt...  3.43 us

profile of v4, /device:TPU:0, one launch (start us, length us, event | category | flops | bytes accessed | tf_op | source)
XLA Modules:
  0.0 65.2 jit_solution(17859658216031540333)
XLA Ops:
  0.6 61.2 %shard_map.76 = (f32[512,4096]{1,0:T(8,128)S(1)}, bf16[16,4096]{1,0:T(8,128)(2,1)S(1)}, f32[1,256]{1,0:T(1,128)S(1)}) custom-call(bf16[1024,4096]{1,0:T(8,128)(2,1)} %table_hbm.1, bf16[16,4096]{1,0:T(8,128)(2,1)} %hidden_hbm.1, bf16[16,4096]{1,0:T(8,128)(2,1)} %cot_hbm.1, s32[1,256]{1,0:T(1,128)} %bitcast.3, s32[1,256]{1,0:T(1,128)} %bitcast.4), custom_call_target="tpu_custom_call" | custom-call | tf_op jit(solution)/shard_map/pallas_call | solution.py:519
  61.8 3.4 %shard_map.77 = (f32[512,4096]{1,0:T(8,128)}, bf16[16,4096]{1,0:T(8,128)(2,1)}, f32[1,256]{1,0:T(1,128)}) custom-call(f32[512,4096]{1,0:T(8,128)S(1)} %get-tuple-element.9.tg_ref, bf16[16,4096]{1,0:T(8,128)(2,1)S(1)} %get-tuple-element.10.hg_ref, f32[1,256]{1,0:T(1,128)S(1)} %get-tuple-element.11.loss_ref), custom_call_target="tpu_custom_call" | custom-call | tf_op jit(solution)/shard_map/pallas_call | solution.py:540
